TPU v7x, 256 devices: a 2x2x32 block of a 4x8x32 slice. The times are simulated.
256 devices in a mesh: groups: 4 (over x, y), row: 64 (over z, core).
Axes of the slice: x: 2, y: 2, z: 32, core: 2. Of those that a mesh axis runs over, the one named last changes fastest.
The devices are a block of a 4x8x32 slice.
Arguments:
- factor_b: bfloat16 [64, 1048576], P(None, ('groups', 'row')), parts along dimension 1, may hold values from -12 to 12
- factor_c: bfloat16 [64, 1048576], P(None, ('groups', 'row')), parts along dimension 1, may hold values from -12 to 12
- sample_j: int32 [2097152], P(('groups', 'row')), parts along dimension 0, may hold values from 0 to 262143, as said below
- sample_k: int32 [64, 256, 128], P(None, ('groups', 'row')), parts along dimension 1, may hold values from 0 to 262143, as said below
- sample_weight: float32 [2097152], P(('groups', 'row')), parts along dimension 0, may hold values from 0.5 to 3.5
- block_values: bfloat16 [256, 64, 4, 4, 128], P(('groups', 'row')), parts along dimension 0, may hold values from -24 to 24
- block_sample: int32 [256, 64, 4, 4], P(('groups', 'row')), parts along dimension 0, may hold values from 0 to 8191
- block_count: int32 [256, 64, 4, 4], P(('groups', 'row')), parts along dimension 0, may hold values from 0 to 128, as said below
Outputs:
- factor_new: bfloat16 [64, 131072], P(None, ('groups', 'row')), parts along dimension 1
- scales: float32 [256], P('groups'), parts along dimension 0
There are 4 independent parts, one for each index of `groups`. A program takes and returns all parts, laid end to end along the dimension named above; each array names one. Nothing has to cross between parts.
Inputs may be any that keep to these rules, and one draw needn't show every extreme that they name: sample_j[s] lies in rows s // 8192 * 4096 to s // 8192 * 4096 + 4095. sample_k[d, e, i] is the third-mode index of sample d * 8192 + e * 128 + i and lies in rows e * 4096 to e * 4096 + 4095. `block_count`: 0 marks an empty slot; slot [p, p, 0, 0] holds 128 for every p.
All inputs are finite; a program needn't handle non-finite values.
Results may differ from a plain program's by a relative error of at most 0.0051.
Values may be sent and summed in bfloat16 or wider, within the bound.
A program may use at most 64 MiB of HBM per device.

v0:
```python
import jax
import jax.numpy as jnp
from jax import lax
from jax.sharding import Mesh
from jax.sharding import PartitionSpec as P

ROW = ("row_0", "row_1")
GROUPS_ROW = ("groups", "row_0", "row_1")


def by_axis(x, axes):
    for axis in axes:
        x = lax.psum(x, axis)
    return x


def sent_together(arrays, axis, split_dim, concat_dim, along):
    both = jnp.concatenate(arrays, axis=along)
    result, at, finished = (
        lax.all_to_all(both, axis, split_axis=split_dim, concat_axis=concat_dim, tiled=True),
        0,
        [],
    )
    for a in arrays:
        finished.append(lax.slice_in_dim(result, at, at + a.shape[along], axis=along))
        at += a.shape[along]
    return tuple(finished)


def from_everyone(x, axis):
    devices = lax.axis_size(axis)
    return lax.all_to_all(jnp.broadcast_to(x[None], (devices, *x.shape)), axis, 0, 0, tiled=True)


def over_copies(x, axis):
    return from_everyone(x, axis).sum(axis=0)


def shards(
    factor_b, factor_c, sample_j, sample_k, sample_weight, block_values, block_sample, block_count
):
    rank_width = factor_b.shape[0]
    device_count = lax.axis_size(ROW)
    device_index = lax.axis_index(ROW)
    b_columns = jnp.take(factor_b, sample_j - device_index * factor_b.shape[1], axis=1)
    c_local = sample_k.reshape(-1) - device_index * factor_c.shape[1]
    c_outgoing = jnp.take(factor_c, c_local, axis=1).reshape(rank_width, device_count, -1)
    c_columns = lax.all_to_all(c_outgoing, ROW, split_axis=1, concat_axis=1, tiled=True).reshape(
        rank_width, -1
    )
    sketch = sample_weight[None, :] * b_columns.astype(jnp.float32) * c_columns.astype(jnp.float32)
    gram_local = jnp.dot(sketch, sketch.T, precision=lax.Precision.HIGHEST)
    live_local = jnp.sum(block_count.astype(jnp.float32))
    gram_matrix, live_total = (by_axis(gram_local, ROW), by_axis(live_local, ROW))
    weighted = (sample_weight[None, :] * sketch).astype(jnp.bfloat16)
    positions = lax.broadcasted_iota(jnp.int32, block_values.shape, 4)
    masked = jnp.where(
        positions < block_count[..., None], block_values, jnp.zeros_like(block_values)
    )[0]
    tile_count = masked.shape[1]
    slot_count = masked.shape[2]
    weighted_rows = weighted.T
    picked = jnp.take(weighted_rows, block_sample.reshape(-1), axis=0)
    picked = picked.reshape(device_count, tile_count, slot_count, rank_width)
    values_in, rows_in = sent_together(
        (masked.reshape(device_count, -1), picked.reshape(device_count, -1)), ROW, 0, 0, 1
    )
    gathered = jnp.einsum(
        "stcr,stck->ktr",
        values_in.reshape(masked.shape),
        rows_in.reshape(picked.shape),
        preferred_element_type=jnp.float32,
    ).reshape(rank_width, -1)
    total_rows = gathered.shape[1] * device_count
    total_samples = sketch.shape[1] * device_count
    ridge = 0.05 * live_total / total_rows
    system = gram_matrix / total_samples + ridge * jnp.eye(rank_width, dtype=jnp.float32)
    lower_factor = jnp.linalg.cholesky(system)
    half_solved = lax.linalg.triangular_solve(lower_factor, gathered, left_side=True, lower=True)
    update = lax.linalg.triangular_solve(
        lower_factor, half_solved, left_side=True, lower=True, transpose_a=True
    )
    column_sums = over_copies(jnp.sum(update * update, axis=1), ROW)
    scales = jnp.sqrt(column_sums / total_rows + 1e-06)
    return ((update / scales[:, None]).astype(jnp.bfloat16), scales)


def solution(mesh):
    split = Mesh(mesh.devices.reshape(mesh.shape["groups"], 32, 2), ("groups", "row_0", "row_1"))
    return jax.shard_map(
        shards,
        mesh=split,
        in_specs=(
            P(None, GROUPS_ROW),
            P(None, GROUPS_ROW),
            P(GROUPS_ROW),
            P(None, GROUPS_ROW, None),
            P(GROUPS_ROW),
            P(GROUPS_ROW, None, None, None, None),
            P(GROUPS_ROW, None, None, None),
            P(GROUPS_ROW, None, None, None),
        ),
        out_specs=(P(None, GROUPS_ROW), P("groups")),
        check_vma=False,
    )
```

profile of v0, /device:TPU:44, one launch (start us, length us, event | category | flops | bytes accessed | tf_op | source)
XLA Modules:
  0.0 407.9 jit_solution(13769192548734777162)
XLA Ops:
  0.6 0.8 broadcast_subtract_fusion
  1.4 1.5 copy.61
  3.0 29.2 %gather_fusion.2 = bf16[8192,64]{1,0:T(8,128)(2,1)} fusion(bf16[64,4096]{0,1:T(8,128)(2,1)S(1)} %copy.61, s32[8192]{0:T(1024)S(1)} %fusion.11), kind=kCustom, calls=%fused_computation.1.clone | custom fusion | bytes 2129920 | tf_op jit(solution)/shard_map/jit(_take)/gather | solution.py:47
  32.2 5.8 %broadcast_select_fusion = bf16[8192,64]{1,0:T(8,128)(2,1)S(1)} fusion(bf16[8192,64]{1,0:T(8,128)(2,1)} %gather_fusion.2, pred[8192]{0:T(1024)(128)(4,1)S(1)} %compare_and_fusion), kind=kLoop, calls=%fused_computation.6 | loop fusion | flops 524288 | bytes 2105344 | tf_op jit(solution)/shard_map/jit(_take)/select_n | solution.py:47
  38.0 0.0 copy-start
  38.0 1.6 copy.62
  39.7 34.4 %all-to-all-start = ((bf16[64,64,128]{2,0,1:T(8,128)(2,1)}), bf16[64,64,128]{2,0,1:T(8,128)(2,1)S(1)}, u32[]{:S(2)}, u32[]{:S(2)}) async-start(bf16[64,64,128]{2,0,1:T(8,128)(2,1)} %copy.62), calls=%async_computation | async-start | bytes 2097152 | tf_op jit(solution)/shard_map/all_to_all | solution.py:48
  74.1 0.0 copy-start.2
  74.1 0.5 copy.60
  74.6 0.1 copy.67
  74.7 0.2 reshape.108
  74.9 0.1 copy.66
  75.0 0.2 broadcast_in_dim.37
  75.2 0.2 broadcast_in_dim.38
  75.4 0.0 copy-done.5
  75.4 0.1 copy.65
  75.6 0.3 fusion.1
  75.9 0.2 reshape_squeeze.3
  76.1 29.2 %gather_fusion.1 = bf16[8192,64]{1,0:T(8,128)(2,1)} fusion(bf16[64,4096]{0,1:T(8,128)(2,1)S(1)} %copy.60, s32[8192]{0:T(1024)S(1)} %fusion.12), kind=kCustom, calls=%fused_computation.clone | custom fusion | bytes 2129920 | tf_op jit(solution)/shard_map/jit(_take)/gather | solution.py:45
  105.4 0.0 copy-start.3
  105.4 77.8 %all-to-all-done = bf16[64,64,128]{2,0,1:T(8,128)(2,1)S(1)} async-done(((bf16[64,64,128]{2,0,1:T(8,128)(2,1)}), bf16[64,64,128]{2,0,1:T(8,128)(2,1)S(1)}, u32[]{:S(2)}, u32[]{:S(2)}) %all-to-all-start) | async-done | bytes 1048608 | tf_op jit(solution)/shard_map/all_to_all | solution.py:48
  183.2 2.4 copy.63
  185.6 10.4 %fusion = (bf16[8192,64]{1,0:T(8,128)(2,1)S(1)}, f32[64,8192]{0,1:T(8,128)}) fusion(f32[8192]{0:T(1024)S(1)} %copy-done.3, f32[64,64,128]{0,2,1:T(8,128)} %copy.63, bf16[8192,64]{1,0:T(8,128)(2,1)} %gather_fusion.1, pred[8192]{0:T(1024)(128)(4,1)S(1)} %compare_and_fusion.1), kind=kLoop, calls=%fused_computation.5 | loop fusion | flops 3145728 | bytes 6332416 | tf_op jit(solution)/shard_map/transpose | solution.py:62
  196.0 3.2 gather_fusion
  199.2 0.2 gather.10
  199.4 0.5 broadcast.154
  200.0 0.9 reduce.7
  200.8 1.0 reshape.144
  201.9 6.7 %all-to-all-start.1 = ((bf16[64,2,1536]{2,1,0:T(2,128)(2,1)}), bf16[64,2,1536]{2,1,0:T(2,128)(2,1)S(1)}, u32[]{:S(2)}, u32[]{:S(2)}) async-start(bf16[64,2,1536]{2,1,0:T(2,128)(2,1)} %reshape.144), calls=%async_computation.1 | async-start | bytes 786432 | tf_op jit(solution)/shard_map/all_to_all | solution.py:20
  208.5 0.6 convert_reduce_fusion
  209.1 10.4 %fusion.13 = f32[64,64]{1,0:T(8,128)S(1)} fusion(f32[64,8192]{0,1:T(8,128)} %get-tuple-element.8), kind=kOutput, calls=%fused_computation.44 | convolution fusion | flops 402653184 | bytes 2113536 | tf_op jit(solution)/shard_map/dot_general | solution.py:52
  219.6 125.4 %all-reduce = (f32[64,64]{1,0:T(8,128)S(1)}, f32[]{:T(128)}) all-reduce(f32[64,64]{1,0:T(8,128)S(1)} %fusion.13, f32[]{:T(128)} %convert_reduce_fusion), channel_id=1, replica_groups=mesh['groups'=4,'row_0'=32,'row_1'=2] {'row_0'}, use_global_device_ids=true, to_apply=%region_0.0 | all-reduce | flops 4097 | bytes 32776 | tf_op jit(solution)/shard_map/psum | solution.py:13
  345.0 4.6 %all-reduce.1 = (f32[64,64]{1,0:T(8,128)S(1)}, f32[]{:T(128)}) all-reduce(f32[64,64]{1,0:T(8,128)S(1)} %get-tuple-element.3, f32[]{:T(128)} %get-tuple-element.4), channel_id=1, replica_groups=mesh['groups'=4,'row_0'=32,'row_1'=2] {'row_1'}, use_global_device_ids=true, to_apply=%region_1.3 | all-reduce | flops 4097 | bytes 32776 | tf_op jit(solution)/shard_map/psum | solution.py:13
  350.2 0.1 copy.64
  350.3 5.8 %cholesky.16 = f32[64,64]{1,0:T(8,128)S(1)} custom-call(f32[64,64]{1,0:T(8,128)S(1)} %fusion.10), custom_call_target="Cholesky" | custom-call | tf_op jit(solution)/shard_map/jit(cholesky)/cholesky | solution.py:78
  356.2 0.6 compare_reduce_fusion
  356.8 0.7 fusion.6
  357.5 4.9 %custom-call.8 = f32[1,64,64]{1,2,0:T(8,128)S(1)} custom-call(f32[1,64,64]{2,1,0:T(8,128)S(1)} %fusion.6), custom_call_target="InvertDiagBlocksLowerTriangular" | custom-call | tf_op jit(solution)/shard_map/triangular_solve | solution.py:80
  362.4 0.0 all-to-all-done.1
  362.4 0.3 reshape.145
  362.8 0.1 copy.83
  363.0 0.2 reshape.110
  363.1 0.2 copy.69
  363.3 0.2 convolution_bitcast_fusion
  363.5 0.3 fusion.3
  363.9 0.4 multiply_reduce_fusion
  364.3 42.9 %all_to_all.23 = f32[64,1,64]{2,1,0:T(1,128)S(1)} all-to-all(f32[64,1,64]{2,1,0:T(1,128)S(1)} %broadcast_in_dim.40), channel_id=1, replica_groups=mesh['groups'=4,'row_0'=32,'row_1'=2] {'row_0','row_1'}, dimensions={0} | all-to-all | bytes 32768 | tf_op jit(solution)/shard_map/all_to_all | solution.py:32
  407.2 0.7 divide_convert_fusion
  (27 shorter events, 0.3 us)
Async XLA Ops:
  38.0 36.0 %copy-start = (bf16[64,4096]{1,0:T(8,128)(2,1)S(1)}, bf16[64,4096]{1,0:T(8,128)(2,1)}, u32[]{:S(2)}) copy-start(bf16[64,4096]{1,0:T(8,128)(2,1)} %param.10) | copy-start | bytes 1572868
  39.7 34.9 %copy-start.4 = (s32[1,64,4,4]{1,3,2,0:T(4,128)S(1)}, s32[1,64,4,4]{1,3,2,0:T(4,128)}, u32[]{:S(2)}) copy-start(s32[1,64,4,4]{1,3,2,0:T(4,128)} %param.16) | copy-start | bytes 12292
  39.7 35.7 %copy-start.5 = (s32[1,64,4,4]{1,3,2,0:T(4,128)S(1)}, s32[1,64,4,4]{1,3,2,0:T(4,128)}, u32[]{:S(2)}) copy-start(s32[1,64,4,4]{1,3,2,0:T(4,128)} %param.17) | copy-start | bytes 12292
  39.7 35.9 %copy-start.1 = (bf16[1,64,4,4,128]{4,3,2,1,0:T(4,128)(2,1)S(1)}, bf16[1,64,4,4,128]{4,3,2,1,0:T(4,128)(2,1)}, u32[]{:S(2)}) copy-start(bf16[1,64,4,4,128]{4,3,2,1,0:T(4,128)(2,1)} %param.15) | copy-start | bytes 786436
  39.7 143.5 %all-to-all-start = ((bf16[64,64,128]{2,0,1:T(8,128)(2,1)}), bf16[64,64,128]{2,0,1:T(8,128)(2,1)S(1)}, u32[]{:S(2)}, u32[]{:S(2)}) async-start(bf16[64,64,128]{2,0,1:T(8,128)(2,1)} %copy.62), calls=%async_computation | async-start | bytes 2097152 | tf_op jit(solution)/shard_map/all_to_all | solution.py:48
  74.1 2.0 copy-start.2
  105.4 80.2 %copy-start.3 = (f32[8192]{0:T(1024)S(1)}, f32[8192]{0:T(1024)}, u32[]{:S(2)}) copy-start(f32[8192]{0:T(1024)} %param.14) | copy-start | bytes 98308
  201.9 160.5 %all-to-all-start.1 = ((bf16[64,2,1536]{2,1,0:T(2,128)(2,1)}), bf16[64,2,1536]{2,1,0:T(2,128)(2,1)S(1)}, u32[]{:S(2)}, u32[]{:S(2)}) async-start(bf16[64,2,1536]{2,1,0:T(2,128)(2,1)} %reshape.144), calls=%async_computation.1 | async-start | bytes 786432 | tf_op jit(solution)/shard_map/all_to_all | solution.py:20
  407.2 0.7 copy-start.6
where the time goes:
time: 409 us; the launch traced here: 408 us
  blocking collectives  173 us (42%)
  waiting for transfers between devices  77.8 us (19%)
  local copies, waits for them, and re-layouts  71.5 us (17%)
  starting transfers between devices  41 us (10%)
  other arithmetic  31.7 us (8%)
  matrix products  11.3 us (3%)
    psum x2, blocking collectives, by_axis(): x = lax.psum(x, axis)  130 us
    all_to_all x1, waiting for transfers between devices, shards(): lax.all_to_all(c_outgoing, ROW, split_axis=1, concat_axis=1, tiled=True)  77.8 us
    all_to_all x1, blocking collectives, from_everyone(): lax.all_to_all(jnp.broadcast_to(x[None], (devices, *x.shape)), axis, 0, 0...  42.9 us
    all_to_all x1, starting transfers between devices, shards(): lax.all_to_all(c_outgoing, ROW, split_axis=1, concat_axis=1, tiled=True)  34.4 us
    gather x1, local copies, waits for them, and re-layouts, shards(): jnp.take(factor_c, c_local, axis=1).reshape(rank_width, device_count, -1)  29.2 us
    gather x1, local copies, waits for them, and re-layouts, shards(): jnp.take(factor_b, sample_j - device_index * factor_b.shape[1], axis=1)  29.2 us
    dot_general x1, matrix products, shards(): gram_local = jnp.dot(sketch, sketch.T, precision=lax.Precision.HIGHEST)  10.4 us
    transpose x1, other arithmetic, shards(): weighted_rows = weighted.T  10.4 us
  transfers between devices with their start and end apart: 2, of which 1 were waited for; matrix products, arithmetic and copies ran while one was open for 13% of the time, Pallas kernels for 0%

commit v1 on v0

--- a/solution.py
+++ b/solution.py
@@ -10,7 +10,8 @@
 
 def by_axis(x, axes):
     for axis in axes:
-        x = lax.psum(x, axis)
+        blocks = lax.all_gather(x, axis)
+        x = jnp.sum(blocks, axis=0)
     return x
 
 

time: 409 us -> 429 us (1.049)
  blocking collectives: 173 us -> 188 us
    psum x2 -> x0, blocking collectives: 130 us -> none  [by_axis(): x = lax.psum(x, axis)]
    unnamed x0 -> x2, blocking collectives: none -> 85.5 us
    all_gather x0 -> x2, blocking collectives: none -> 60.1 us  [by_axis(): blocks = lax.all_gather(x, axis)]
  transfers between devices with their start and end apart: 2 -> 2, of which waited for: 1 -> 1; matrix products, arithmetic and copies ran while one was open for 13% -> 14% of each run, Pallas kernels for 0% -> 0%
where the time goes in v1:
time: 429 us
  blocking collectives  188 us (44%)
  waiting for transfers between devices  77.8 us (18%)
  local copies, waits for them, and re-layouts  75.5 us (18%)
  starting transfers between devices  40.8 us (10%)
  other arithmetic  33 us (8%)
  matrix products  11.3 us (3%)
    unnamed x2, blocking collectives  85.5 us
    all_to_all x1, waiting for transfers between devices, shards(): lax.all_to_all(c_outgoing, ROW, split_axis=1, concat_axis=1, tiled=True)  77.8 us
    all_gather x2, blocking collectives, by_axis(): blocks = lax.all_gather(x, axis)  60.1 us
    all_to_all x1, blocking collectives, from_everyone(): lax.all_to_all(jnp.broadcast_to(x[None], (devices, *x.shape)), axis, 0, 0...  42.6 us
    all_to_all x1, starting transfers between devices, shards(): lax.all_to_all(c_outgoing, ROW, split_axis=1, concat_axis=1, tiled=True)  34.4 us
    gather x1, local copies, waits for them, and re-layouts, shards(): jnp.take(factor_c, c_local, axis=1).reshape(rank_width, device_count, -1)  29.2 us
    gather x1, local copies, waits for them, and re-layouts, shards(): jnp.take(factor_b, sample_j - device_index * factor_b.shape[1], axis=1)  29.2 us
    dot_general x1, matrix products, shards(): gram_local = jnp.dot(sketch, sketch.T, precision=lax.Precision.HIGHEST)  10.4 us
  transfers between devices with their start and end apart: 2, of which 1 were waited for; matrix products, arithmetic and copies ran while one was open for 14% of the time, Pallas kernels for 0%

profile of v1, /device:TPU:44, one launch (start us, length us, event | category | flops | bytes accessed | tf_op | source)
XLA Modules:
  0.0 428.5 jit_solution(14390687176545572438)
XLA Ops:
  0.6 0.8 broadcast_subtract_fusion
  1.4 1.5 copy.62
  3.0 29.2 %gather_fusion.2 = bf16[8192,64]{1,0:T(8,128)(2,1)} fusion(bf16[64,4096]{0,1:T(8,128)(2,1)S(1)} %copy.62, s32[8192]{0:T(1024)S(1)} %fusion.12), kind=kCustom, calls=%fused_computation.1.clone | custom fusion | bytes 2129920 | tf_op jit(solution)/shard_map/jit(_take)/gather | solution.py:48
  32.2 5.8 %broadcast_select_fusion = bf16[8192,64]{1,0:T(8,128)(2,1)S(1)} fusion(bf16[8192,64]{1,0:T(8,128)(2,1)} %gather_fusion.2, pred[8192]{0:T(1024)(128)(4,1)S(1)} %compare_and_fusion), kind=kLoop, calls=%fused_computation.6 | loop fusion | flops 524288 | bytes 2105344 | tf_op jit(solution)/shard_map/jit(_take)/select_n | solution.py:48
  38.0 1.6 copy.63
  39.7 34.4 %all-to-all-start = ((bf16[64,64,128]{2,0,1:T(8,128)(2,1)}), bf16[64,64,128]{2,0,1:T(8,128)(2,1)S(1)}, u32[]{:S(2)}, u32[]{:S(2)}) async-start(bf16[64,64,128]{2,0,1:T(8,128)(2,1)} %copy.63), calls=%async_computation | async-start | bytes 2097152 | tf_op jit(solution)/shard_map/all_to_all | solution.py:49
  74.1 0.5 copy.61
  74.6 0.1 copy.69
  74.7 0.2 reshape.108
  75.0 0.2 broadcast_in_dim.37
  75.2 0.2 broadcast_in_dim.38
  75.6 0.3 fusion.1
  75.9 0.2 reshape_squeeze.3
  76.1 29.2 %gather_fusion.1 = bf16[8192,64]{1,0:T(8,128)(2,1)} fusion(bf16[64,4096]{0,1:T(8,128)(2,1)S(1)} %copy.61, s32[8192]{0:T(1024)S(1)} %fusion.13), kind=kCustom, calls=%fused_computation.clone | custom fusion | bytes 2129920 | tf_op jit(solution)/shard_map/jit(_take)/gather | solution.py:46
  105.4 77.8 %all-to-all-done = bf16[64,64,128]{2,0,1:T(8,128)(2,1)S(1)} async-done(((bf16[64,64,128]{2,0,1:T(8,128)(2,1)}), bf16[64,64,128]{2,0,1:T(8,128)(2,1)S(1)}, u32[]{:S(2)}, u32[]{:S(2)}) %all-to-all-start) | async-done | bytes 1048608 | tf_op jit(solution)/shard_map/all_to_all | solution.py:49
  183.2 2.4 copy.64
  185.6 10.4 %fusion = (bf16[8192,64]{1,0:T(8,128)(2,1)S(1)}, f32[64,8192]{0,1:T(8,128)}) fusion(f32[8192]{0:T(1024)S(1)} %copy-done.3, f32[64,64,128]{0,2,1:T(8,128)} %copy.64, bf16[8192,64]{1,0:T(8,128)(2,1)} %gather_fusion.1, pred[8192]{0:T(1024)(128)(4,1)S(1)} %compare_and_fusion.1), kind=kLoop, calls=%fused_computation.5 | loop fusion | flops 3145728 | bytes 6332416 | tf_op jit(solution)/shard_map/transpose | solution.py:63
  196.0 3.2 gather_fusion
  199.2 0.2 gather.10
  199.5 0.5 broadcast.159
  200.0 0.9 reduce.9
  200.9 1.0 reshape.156
  201.9 6.5 %all-to-all-start.1 = ((bf16[64,2,1536]{2,1,0:T(2,128)(2,1)}), bf16[64,2,1536]{2,1,0:T(2,128)(2,1)S(1)}, u32[]{:S(2)}, u32[]{:S(2)}) async-start(bf16[64,2,1536]{2,1,0:T(2,128)(2,1)} %reshape.156), calls=%async_computation.1 | async-start | bytes 786432 | tf_op jit(solution)/shard_map/all_to_all | solution.py:21
  208.4 0.6 dynamic-slice
  209.0 0.6 convert_reduce_fusion
  209.6 1.4 dynamic-update-slice.3
  211.0 82.9 %all-reduce = f32[32]{0:T(128)S(1)} all-reduce(f32[32]{0:T(128)S(1)} %dynamic-update-slice.3), channel_id=1, replica_groups=mesh['groups'=4,'row_0'=32,'row_1'=2] {'row_0'}, use_global_device_ids=true, to_apply=%add | all-reduce | flops 32 | bytes 256
  293.9 0.6 reduce_sum.66
  294.5 0.6 dynamic-slice.1
  295.0 1.4 dynamic-update-slice.4
  296.5 2.7 all-reduce.1
  299.1 0.6 reduce_sum.67
  300.4 10.4 %fusion.14 = f32[64,64]{1,0:T(8,128)S(1)} fusion(f32[64,8192]{0,1:T(8,128)} %get-tuple-element.4), kind=kOutput, calls=%fused_computation.46 | convolution fusion | flops 402653184 | bytes 2113536 | tf_op jit(solution)/shard_map/dot_general | solution.py:53
  310.8 58.2 %all-gather = f32[2048,64]{1,0:T(8,128)S(1)} all-gather(f32[64,64]{1,0:T(8,128)S(1)} %fusion.14), channel_id=2, replica_groups=mesh['groups'=4,'row_0'=32,'row_1'=2] {'row_0'}, dimensions={0}, use_global_device_ids=true | all-gather | bytes 540672 | tf_op jit(solution)/shard_map/all_gather | solution.py:13
  369.1 1.9 all-gather.1
  371.2 5.8 %cholesky.16 = f32[64,64]{1,0:T(8,128)S(1)} custom-call(f32[64,64]{1,0:T(8,128)S(1)} %fusion.11), custom_call_target="Cholesky" | custom-call | tf_op jit(solution)/shard_map/jit(cholesky)/cholesky | solution.py:79
  377.1 0.6 compare_reduce_fusion
  377.7 0.7 fusion.6
  378.4 4.9 %custom-call.8 = f32[1,64,64]{1,2,0:T(8,128)S(1)} custom-call(f32[1,64,64]{2,1,0:T(8,128)S(1)} %fusion.6), custom_call_target="InvertDiagBlocksLowerTriangular" | custom-call | tf_op jit(solution)/shard_map/triangular_solve | solution.py:81
  383.3 0.3 reshape.157
  383.7 0.1 copy.85
  383.8 0.2 reshape.110
  384.0 0.2 copy.71
  384.2 0.2 convolution_bitcast_fusion
  384.4 0.3 fusion.3
  384.8 0.4 multiply_reduce_fusion
  385.1 42.6 %all_to_all.23 = f32[64,1,64]{2,1,0:T(1,128)S(1)} all-to-all(f32[64,1,64]{2,1,0:T(1,128)S(1)} %broadcast_in_dim.40), channel_id=1, replica_groups=mesh['groups'=4,'row_0'=32,'row_1'=2] {'row_0','row_1'}, dimensions={0} | all-to-all | bytes 32768 | tf_op jit(solution)/shard_map/all_to_all | solution.py:33
  427.8 0.7 divide_convert_fusion
  (44 shorter events, 0.8 us)
Async XLA Ops:
  38.0 36.0 %copy-start = (bf16[64,4096]{1,0:T(8,128)(2,1)S(1)}, bf16[64,4096]{1,0:T(8,128)(2,1)}, u32[]{:S(2)}) copy-start(bf16[64,4096]{1,0:T(8,128)(2,1)} %param.10) | copy-start | bytes 1572868
  39.7 34.9 %copy-start.4 = (s32[1,64,4,4]{1,3,2,0:T(4,128)S(1)}, s32[1,64,4,4]{1,3,2,0:T(4,128)}, u32[]{:S(2)}) copy-start(s32[1,64,4,4]{1,3,2,0:T(4,128)} %param.16) | copy-start | bytes 12292
  39.7 35.7 %copy-start.5 = (s32[1,64,4,4]{1,3,2,0:T(4,128)S(1)}, s32[1,64,4,4]{1,3,2,0:T(4,128)}, u32[]{:S(2)}) copy-start(s32[1,64,4,4]{1,3,2,0:T(4,128)} %param.17) | copy-start | bytes 12292
  39.7 35.9 %copy-start.1 = (bf16[1,64,4,4,128]{4,3,2,1,0:T(4,128)(2,1)S(1)}, bf16[1,64,4,4,128]{4,3,2,1,0:T(4,128)(2,1)}, u32[]{:S(2)}) copy-start(bf16[1,64,4,4,128]{4,3,2,1,0:T(4,128)(2,1)} %param.15) | copy-start | bytes 786436
  39.7 143.5 %all-to-all-start = ((bf16[64,64,128]{2,0,1:T(8,128)(2,1)}), bf16[64,64,128]{2,0,1:T(8,128)(2,1)S(1)}, u32[]{:S(2)}, u32[]{:S(2)}) async-start(bf16[64,64,128]{2,0,1:T(8,128)(2,1)} %copy.63), calls=%async_computation | async-start | bytes 2097152 | tf_op jit(solution)/shard_map/all_to_all | solution.py:49
  74.1 2.0 copy-start.2
  105.4 80.2 %copy-start.3 = (f32[8192]{0:T(1024)S(1)}, f32[8192]{0:T(1024)}, u32[]{:S(2)}) copy-start(f32[8192]{0:T(1024)} %param.14) | copy-start | bytes 98308
  199.2 9.2 %copy-start.8 = (u32[256]{0:T(256)S(1)}, u32[256]{0:T(256)}, u32[]{:S(2)}) copy-start(u32[256]{0:T(256)} %constant.106) | copy-start | bytes 3076
  199.2 95.3 %copy-start.7 = (u32[256]{0:T(256)S(1)}, u32[256]{0:T(256)}, u32[]{:S(2)}) copy-start(u32[256]{0:T(256)} %constant.111) | copy-start | bytes 3076
  201.9 181.4 %all-to-all-start.1 = ((bf16[64,2,1536]{2,1,0:T(2,128)(2,1)}), bf16[64,2,1536]{2,1,0:T(2,128)(2,1)S(1)}, u32[]{:S(2)}, u32[]{:S(2)}) async-start(bf16[64,2,1536]{2,1,0:T(2,128)(2,1)} %reshape.156), calls=%async_computation.1 | async-start | bytes 786432 | tf_op jit(solution)/shard_map/all_to_all | solution.py:21
  427.8 0.7 copy-start.6
